TPU v7x, 256 devices: a 8x8x2 block of a 8x8x16 slice. The times are simulated.
256 devices in a mesh: groups: 2 (over z), seq: 64 (over x, y), mp: 2 (over core).
Axes of the slice: x: 8, y: 8, z: 2, core: 2. Of those that a mesh axis runs over, the one named last changes fastest.
The devices are a block of a 8x8x16 slice.
Arguments:
- latent_cache: bfloat16 [16384, 64, 512], P(('groups', 'seq')), parts along dimension 0, may hold values from -6 to 6
- rope_cache: bfloat16 [16384, 4096], P(('groups', 'seq')), parts along dimension 0, may hold values from -6 to 6
- q_nope: bfloat16 [16, 128, 128], P('groups', 'mp'), parts along dimension 0, may hold values from -12 to 12
- q_rope: bfloat16 [16, 128, 64], P('groups', 'mp'), parts along dimension 0, may hold values from -2000 to 2000
- w_uk: bfloat16 [128, 128, 512], P('mp', None, 'seq'), may hold values from -0.5 to 0.5
- value_up_weight: bfloat16 [128, 512, 128], P('mp', 'seq'), may hold values from -0.25 to 0.25
- w_out: bfloat16 [16384, 7168], P('mp', 'seq'), may hold values from -0.046875 to 0.046875
- page_table: int32 [16, 2048], P('groups'), parts along dimension 0, may hold values from 0 to 8191, as said below
- lengths: int32 [16], P('groups'), parts along dimension 0, may hold values from 16384 to 131072, as said below
Outputs:
- output: bfloat16 [16, 7168], P('groups', ('seq', 'mp')), parts along dimension 0
There are 2 independent parts, one for each index of `groups`. A program takes and returns all parts, laid end to end along the dimension named above; an argument that names none is the same for every part. Nothing has to cross between parts.
Inputs may be any that keep to these rules, and one draw needn't show every extreme that they name: `lengths`: every sequence has one eighth of 131072 tokens or more; the longest has exactly 131072. page_table[b,p] for p < ceil(lengths[b] / 64) is the global slot (shard index times 128 plus local slot) holding that page; these live entries are all distinct; the other entries are 0 and unused.
All inputs are finite; a program needn't handle non-finite values.
Results may differ from a plain program's by a relative error of at most 0.012.
Values may be sent and summed in bfloat16 or wider, within the bound.
A program may use at most 64 MiB of HBM per device.

v0:
```python
import jax
import jax.numpy as jnp
from jax import lax
from jax.sharding import Mesh
from jax.sharding import PartitionSpec as P

SEQ = ("seq_0", "seq_1")
GROUPS_SEQ = ("groups", "seq_0", "seq_1")
SEQ_MP = ("seq_0", "seq_1", "mp")
NEG = -1e30


def laid_out(tiles, dim):
    tiles = jnp.moveaxis(tiles, 0, dim)
    lengths = tiles.shape
    return tiles.reshape(*lengths[:dim], lengths[dim] * lengths[dim + 1], *lengths[dim + 2 :])


def from_everyone(x, axis):
    size = lax.axis_size(axis)
    return lax.all_to_all(jnp.broadcast_to(x[None], (size, *x.shape)), axis, 0, 0, tiled=True)


def collect(x, axis, dim):
    return laid_out(from_everyone(x, axis), dim)


def side_by_side(arrays, axis, split_dim, concat_dim, along):
    ends, at = ([], 0)
    for a in arrays[:-1]:
        at += a.shape[along]
        ends.append(at)
    both = jnp.concatenate(arrays, axis=along)
    return tuple(
        jnp.split(
            lax.all_to_all(both, axis, split_axis=split_dim, concat_axis=concat_dim, tiled=True),
            ends,
            axis=along,
        )
    )


def by_axis(x, axes):
    for axis in axes:
        x = lax.psum(x, axis)
    return x


def cut_along(x, dim, size):
    lengths = x.shape
    tiles = x.reshape(*lengths[:dim], size, lengths[dim] // size, *lengths[dim + 1 :])
    return jnp.moveaxis(tiles, dim, 0)


def sum_at_owner(x, axis, dim):
    size = lax.axis_size(axis)
    tiles = lax.all_to_all(cut_along(x, dim, size), axis, 0, 0, tiled=True)
    return jnp.sum(tiles, axis=0)


def local(
    latent_cache, rope_cache, q_nope, q_rope, w_uk, value_up_weight, w_out, page_table, lengths
):
    slots_dev, page_len, latent_width = latent_cache.shape
    rope_width = q_rope.shape[2]
    seq_count, heads = (q_nope.shape[0], q_nope.shape[1])
    score_scale = (q_nope.shape[2] + rope_width) ** (-0.5)
    q_part = jnp.einsum("bhn,hnk->bhk", q_nope, w_uk, preferred_element_type=jnp.float32).astype(
        jnp.bfloat16
    )
    q_latent = collect(q_part, SEQ, 2)
    first_slot = lax.axis_index(SEQ) * slots_dev
    page_count = (lengths + page_len - 1) // page_len
    logical = jnp.arange(page_table.shape[1], dtype=jnp.int32)
    live_page = logical[None, :] < page_count[:, None]
    tokens_in = jnp.clip(lengths[:, None] - page_len * logical[None, :], 0, page_len)
    local_ids = jnp.arange(slots_dev, dtype=jnp.int32)
    hits = ((page_table - first_slot)[:, :, None] == local_ids[None, None, :]) & live_page[
        :, :, None
    ]
    owner_mask = jnp.any(hits, axis=1)
    slot_fill = jnp.sum(jnp.where(hits, tokens_in[:, :, None], 0), axis=(0, 1))
    owner_half = owner_mask.astype(jnp.bfloat16)

    def update(run_state, index):
        run_max, run_sum, run_out = run_state
        start = index * 8
        latent_block = lax.dynamic_slice_in_dim(latent_cache, start, 8, 0)
        rope_block = lax.dynamic_slice_in_dim(rope_cache, start, 8, 0).reshape(
            8, page_len, rope_width
        )
        owner_block = lax.dynamic_slice_in_dim(owner_half, start, 8, 1)
        fill_block = lax.dynamic_slice_in_dim(slot_fill, start, 8, 0)
        pick_latent = jnp.einsum(
            "bs,bhk->shk", owner_block, q_latent, preferred_element_type=jnp.float32
        ).astype(jnp.bfloat16)
        pick_rope = jnp.einsum(
            "bs,bhr->shr", owner_block, q_rope, preferred_element_type=jnp.float32
        ).astype(jnp.bfloat16)
        scores = (
            jnp.einsum(
                "shk,stk->sht", pick_latent, latent_block, preferred_element_type=jnp.float32
            )
            + jnp.einsum("shr,str->sht", pick_rope, rope_block, preferred_element_type=jnp.float32)
        ) * score_scale
        live_token = (
            jnp.arange(page_len, dtype=jnp.int32)[None, None, :] < fill_block[:, None, None]
        )
        slot_max = jnp.max(jnp.where(live_token, scores, NEG), axis=2)
        exponent = jnp.where(live_token, jnp.exp(scores - slot_max[:, :, None]), 0.0)
        slot_sum = jnp.sum(exponent, axis=2)
        slot_out = jnp.einsum(
            "sht,stk->shk",
            exponent.astype(jnp.bfloat16),
            latent_block,
            preferred_element_type=jnp.float32,
        )
        owned = owner_block > 0
        candidate = jnp.where(owned[:, :, None], slot_max[None, :, :], NEG)
        new_max = jnp.maximum(run_max, jnp.max(candidate, axis=1))
        carry_scale = jnp.exp(run_max - new_max)
        factor = jnp.where(owned[:, :, None], jnp.exp(candidate - new_max[:, None, :]), 0.0)
        run_sum = run_sum * carry_scale + jnp.einsum("bsh,sh->bh", factor, slot_sum)
        run_out = run_out * carry_scale[:, :, None] + jnp.einsum("bsh,shk->bhk", factor, slot_out)
        return (new_max, run_sum, run_out)

    def visit(index, run_state):
        return update(run_state, index)

    initial = (
        jnp.full((seq_count, heads), NEG, jnp.float32),
        jnp.zeros((seq_count, heads), jnp.float32),
        jnp.zeros((seq_count, heads, latent_width), jnp.float32),
    )
    run_max, run_sum, run_out = lax.fori_loop(0, slots_dev // 8, visit, initial)
    share_width = value_up_weight.shape[1]
    shards = lax.axis_size(SEQ)
    spread_max = jnp.broadcast_to(run_max[:, :, None], (seq_count, heads, shards))
    spread_sum = jnp.broadcast_to(run_sum[:, :, None], (seq_count, heads, shards))
    peers_max, peers_sum, peers_out = (
        *side_by_side((spread_max, spread_sum), SEQ, 2, 2, 0),
        lax.all_to_all(run_out, SEQ, split_axis=2, concat_axis=2, tiled=True),
    )
    top = jnp.max(peers_max, axis=2)
    rescale = jnp.exp(peers_max - top[:, :, None])
    totals = jnp.sum(peers_sum * rescale, axis=2)
    grouped = peers_out.reshape(seq_count, heads, shards, share_width)
    shared_latent = jnp.sum(grouped * rescale[:, :, :, None], axis=2)
    local_portion = (shared_latent / totals[:, :, None]).astype(jnp.bfloat16)
    value_slice = jnp.einsum(
        "gre,req->grq", local_portion, value_up_weight, preferred_element_type=jnp.float32
    )
    value_rows = by_axis(value_slice, SEQ).astype(jnp.bfloat16)
    flat_values = value_rows.reshape(seq_count, heads * value_rows.shape[2])
    partial_out = jnp.dot(flat_values, w_out, preferred_element_type=jnp.float32)
    return sum_at_owner(partial_out, "mp", 1).astype(jnp.bfloat16)


def solution(mesh):
    finer = Mesh(
        mesh.devices.reshape(mesh.shape["groups"], 8, 8, mesh.shape["mp"]),
        ("groups", "seq_0", "seq_1", "mp"),
    )
    return jax.shard_map(
        local,
        mesh=finer,
        in_specs=(
            P(GROUPS_SEQ, None, None),
            P(GROUPS_SEQ, None),
            P("groups", "mp", None),
            P("groups", "mp", None),
            P("mp", None, SEQ),
            P("mp", SEQ, None),
            P("mp", SEQ),
            P("groups", None),
            P("groups"),
        ),
        out_specs=P("groups", SEQ_MP),
        check_vma=False,
    )
```

profile of v0, /device:TPU:513, one launch (start us, length us, event | category | flops | bytes accessed | tf_op | source)
XLA Modules:
  0.0 388.7 jit_solution(2890915873763073449)
XLA Ops:
  9.8 21.8 %all-to-all-start = ((bf16[64,2,2048]{2,1,0:T(2,128)(2,1)}), bf16[64,2,2048]{2,1,0:T(2,128)(2,1)}, u32[]{:S(2)}, u32[]{:S(2)}) async-start(bf16[64,2,2048]{2,1,0:T(2,128)(2,1)} %reshape.114), calls=%async_computation | async-start | bytes 1048576 | tf_op jit(solution)/shard_map/all_to_all | solution.py:21
  31.9 5.7 %fusion.41 = pred[8,128]{1,0:T(8,128)(4,1)S(1)} fusion(s32[8,2048]{1,0:T(8,128)S(1)} %get-tuple-element.269, pred[8,2048]{1,0:T(8,128)(4,1)S(1)} %iota_compare_fusion.2), kind=kLoop, calls=%fused_computation.56 | loop fusion | flops 6290432 | bytes 82944 | tf_op jit(solution)/shard_map/reduce_or | solution.py:81
  37.7 7.8 %select_reduce_fusion.2 = s32[128]{0:T(128)S(1)} fusion(s32[8,2048]{1,0:T(8,128)S(1)} %get-tuple-element.268, s32[8,2048]{1,0:T(8,128)S(1)} %get-tuple-element.269, pred[8,2048]{1,0:T(8,128)(4,1)S(1)} %iota_compare_fusion.2), kind=kLoop, calls=%fused_computation.53 | loop fusion | flops 8388480 | bytes 147968 | tf_op jit(solution)/shard_map/reduce_sum | solution.py:82
  45.5 2.3 reshape.115
  51.0 138.7 %while.18 = (s32[]{:T(128)}, f32[8,64]{0,1:T(8,128)S(1)}, f32[8,64]{0,1:T(8,128)S(1)}, f32[8,64,512]{2,0,1:T(8,128)}, bf16[8,128]{1,0:T(8,128)(2,1)S(1)}, /*inde...) while((s32[]{:T(128)}, f32[8,64]{0,1:T(8,128)S(1)}, ...), condition=%wide.region_6.7_spmd.clone, body=%wide.region_2.6_spmd.clone.sunk | while | flops 81668672 | bytes 7003699 | solution.py:135
  64.5 2.7 fusion.94
  73.3 2.7 fusion.94
  82.0 2.7 fusion.94
  90.8 2.7 fusion.94
  99.5 2.7 fusion.94
  108.2 2.7 fusion.94
  117.0 2.7 fusion.94
  125.7 2.7 fusion.94
  134.5 2.7 fusion.94
  143.2 2.7 fusion.94
  151.9 2.7 fusion.94
  160.7 2.7 fusion.94
  169.4 2.7 fusion.94
  178.2 2.7 fusion.94
  186.9 2.7 fusion.94
  190.9 13.3 %all-to-all-start.2 = ((f32[64,1,1024]{2,1,0:T(1,128)}), f32[64,1,1024]{2,1,0:T(1,128)S(1)}, u32[]{:S(2)}, u32[]{:S(2)}) async-start(f32[64,1,1024]{2,1,0:T(1,128)} %reshape.118), calls=%async_computation.2 | async-start | bytes 524288 | tf_op jit(solution)/shard_map/all_to_all | solution.py:36
  204.3 2.3 copy.50
  206.6 3.4 reshape.116
  210.0 5.1 %all-to-all-done.2 = f32[64,1,1024]{2,1,0:T(1,128)S(1)} async-done(((f32[64,1,1024]{2,1,0:T(1,128)}), f32[64,1,1024]{2,1,0:T(1,128)S(1)}, u32[]{:S(2)}, u32[]{:S(2)}) %all-to-all-start.2) | async-done | bytes 262176 | tf_op jit(solution)/shard_map/all_to_all | solution.py:36
  215.2 7.9 %all-to-all-start.1 = ((f32[64,1,4096]{2,1,0:T(1,128)}), f32[64,1,4096]{2,1,0:T(1,128)}, u32[]{:S(2)}, u32[]{:S(2)}) async-start(f32[64,1,4096]{2,1,0:T(1,128)} %reshape.116), calls=%async_computation.1 | async-start | bytes 2097152 | tf_op jit(solution)/shard_map/all_to_all | solution.py:142
  225.3 18.9 %all-to-all-done.1 = f32[64,1,4096]{2,1,0:T(1,128)} async-done(((f32[64,1,4096]{2,1,0:T(1,128)}), f32[64,1,4096]{2,1,0:T(1,128)}, u32[]{:S(2)}, u32[]{:S(2)}) %all-to-all-start.1) | async-done | bytes 1048608 | tf_op jit(solution)/shard_map/all_to_all | solution.py:142
  244.2 4.4 %reduce = f32[64,4096]{1,0:T(8,128)S(1)} reduce(f32[64,1,4096]{2,1,0:T(1,128)} %all-to-all-done.1, f32[]{:T(128)} %broadcast.134), dimensions={1}, to_apply=%all_to_all.13.reduce_sub_computation | reduce | bytes 2097156 | tf_op jit(solution)/shard_map/all_to_all | solution.py:142
  248.6 2.2 reshape.117
  250.7 2.2 fusion.42
  254.1 82.6 %all-reduce.3.cloned.1.call-done = f32[8,64,128]{2,0,1:T(8,128)} async-done(((f32[8,64,128]{2,0,1:T(8,128)}), f32[8,64,128]{2,0,1:T(8,128)}) %all-reduce.3.cloned.1.call-update) | async-done | bytes 262160 | tf_op jit(solution)/shard_map/psum | solution.py:45
  336.7 26.8 %all-reduce.4 = bf16[8,64,128]{2,0,1:T(8,128)(2,1)S(1)} all-reduce(f32[8,64,128]{2,0,1:T(8,128)} %all-reduce.3.cloned.1.call-done), channel_id=1, replica_groups=mesh['groups'=2,'seq_0'=8,'seq_1'=8,'mp'=2] {'seq_1'}, use_global_device_ids=true, to_apply=%region_11.12 | all-reduce | flops 65536 | bytes 393216 | tf_op jit(solution)/shard_map/psum | solution.py:45
  364.5 16.0 %all_to_all.20 = f32[2,1,448]{2,1,0:T(1,128)S(1)} all-to-all(f32[2,1,448]{2,1,0:T(1,128)S(1)} %reshape.120), channel_id=1, replica_groups=mesh['groups'=2,'seq_0'=8,'seq_1'=8,'mp'=2] {'mp'}, dimensions={0} | all-to-all | bytes 7168 | tf_op jit(solution)/shard_map/all_to_all | solution.py:57
  (387 shorter events, 110.1 us)
Async XLA Ops:
  6.5 356.9 %copy-start = (bf16[8192,112]{0,1:T(8,128)(2,1)S(1)}, bf16[8192,112]{0,1:T(8,128)(2,1)}, u32[]{:S(2)}) copy-start(bf16[8192,112]{0,1:T(8,128)(2,1)} %param.17) | copy-start | bytes 5505028
  6.6 25.2 %copy-start.5 = (s32[8]{0:T(128)S(1)}, s32[8]{0:T(128)}, u32[]{:S(2)}) copy-start(s32[8]{0:T(128)} %param.19) | copy-start | bytes 100
  6.6 25.2 %copy-start.4 = (s32[8,2048]{1,0:T(8,128)S(1)}, s32[8,2048]{1,0:T(8,128)}, u32[]{:S(2)}) copy-start(s32[8,2048]{1,0:T(8,128)} %param.18) | copy-start | bytes 196612
  7.9 29.8 %copy-start.2 = (bf16[8,64,64]{2,1,0:T(8,128)(2,1)S(1)}, bf16[8,64,64]{2,1,0:T(8,128)(2,1)}, u32[]{:S(2)}) copy-start(bf16[8,64,64]{2,1,0:T(8,128)(2,1)} %param.14) | copy-start | bytes 196612
  9.8 35.7 %all-to-all-start = ((bf16[64,2,2048]{2,1,0:T(2,128)(2,1)}), bf16[64,2,2048]{2,1,0:T(2,128)(2,1)}, u32[]{:S(2)}, u32[]{:S(2)}) async-start(bf16[64,2,2048]{2,1,0:T(2,128)(2,1)} %reshape.114), calls=%async_computation | async-start | bytes 1048576 | tf_op jit(solution)/shard_map/all_to_all | solution.py:21
  189.6 14.6 %copy-start.1 = (f32[8,64,512]{2,0,1:T(8,128)S(1)}, f32[8,64,512]{2,0,1:T(8,128)}, u32[]{:S(2)}) copy-start(f32[8,64,512]{2,0,1:T(8,128)} %get-tuple-element.176) | copy-start | bytes 3145732
  190.9 24.2 %all-to-all-start.2 = ((f32[64,1,1024]{2,1,0:T(1,128)}), f32[64,1,1024]{2,1,0:T(1,128)S(1)}, u32[]{:S(2)}, u32[]{:S(2)}) async-start(f32[64,1,1024]{2,1,0:T(1,128)} %reshape.118), calls=%async_computation.2 | async-start | bytes 524288 | tf_op jit(solution)/shard_map/all_to_all | solution.py:36
  215.2 29.0 %all-to-all-start.1 = ((f32[64,1,4096]{2,1,0:T(1,128)}), f32[64,1,4096]{2,1,0:T(1,128)}, u32[]{:S(2)}, u32[]{:S(2)}) async-start(f32[64,1,4096]{2,1,0:T(1,128)} %reshape.116), calls=%async_computation.1 | async-start | bytes 2097152 | tf_op jit(solution)/shard_map/all_to_all | solution.py:142
  223.1 113.6 %all-reduce.3.cloned.1.call-start = ((), (), s32[]{:S(2)}) async-start(), calls=%async_computation.4 | async-start | bytes 524288 | tf_op jit(solution)/shard_map/psum | solution.py:45
  248.5 4.5 %copy-start.3 = (bf16[64,8,128]{2,1,0:T(8,128)(2,1)S(1)}, bf16[64,8,128]{2,1,0:T(8,128)(2,1)}, u32[]{:S(2)}) copy-start(bf16[64,8,128]{2,1,0:T(8,128)(2,1)} %param.16) | copy-start | bytes 393220
Sparse Core Ops, SparseCore 0:
  254.2 82.4 all-reduce.2
where the time goes:
time: 392 us; the launch traced here: 389 us
  matrix products  110 us (28%)
  waiting for transfers between devices  107 us (27%)
  starting transfers between devices  43.1 us (11%)
  blocking collectives  42.8 us (11%)
  local copies, waits for them, and re-layouts  42.3 us (11%)
  other arithmetic  29.5 us (8%)
  between operations  13.7 us (3%)
    psum x1, waiting for transfers between devices, by_axis(): x = lax.psum(x, axis)  82.6 us
    dot_general x16, matrix products, update(): jnp.einsum('bsh,shk->bhk', factor, slot_out)  42.6 us
    psum x1, blocking collectives, by_axis(): x = lax.psum(x, axis)  26.8 us
    dot_general x16, matrix products, update(): jnp.einsum('sht,stk->shk', exponent.astype(jnp.bfloat16), latent_block, p...  24.3 us
    dot_general x16, matrix products, update(): jnp.einsum('shk,stk->sht', pick_latent, latent_block, preferred_element_t...  22 us
    all_to_all x1, starting transfers between devices, from_everyone(): lax.all_to_all(jnp.broadcast_to(x[None], (size, *x.shape)), axis, 0, 0, t...  21.8 us
    all_to_all x1, waiting for transfers between devices, local(): lax.all_to_all(run_out, SEQ, split_axis=2, concat_axis=2, tiled=True)  18.9 us
    all_to_all x1, blocking collectives, sum_at_owner(): tiles = lax.all_to_all(cut_along(x, dim, size), axis, 0, 0, tiled=True)  16 us
  transfers between devices with their start and end apart: 4, of which 3 were waited for; matrix products, arithmetic and copies ran while one was open for 6% of the time, Pallas kernels for 0%

commit v1 on v0

--- a/solution.py
+++ b/solution.py
@@ -42,7 +42,7 @@
 
 def by_axis(x, axes):
     for axis in axes:
-        x = lax.psum(x, axis)
+        x = jnp.sum(lax.all_gather(x, axis), axis=0)
     return x
 
 

time: 392 us -> 378 us (0.964)
  blocking collectives: 42.8 us -> 8.23 us
  waiting for transfers between devices: 107 us -> 123 us
    all_gather x0 -> x2, waiting for transfers between devices: none -> 98.4 us  [by_axis(): x = jnp.sum(lax.all_gather(x, axis), axis=0)]
    psum x1 -> x0, waiting for transfers between devices: 82.6 us -> none  [by_axis(): x = lax.psum(x, axis)]
    psum x1 -> x0, blocking collectives: 26.8 us -> none  [by_axis(): x = lax.psum(x, axis)]
    all_to_all x1, blocking collectives: 16 us -> 8.23 us  [sum_at_owner(): tiles = lax.all_to_all(cut_along(x, dim, size), axis, 0, 0, tiled=True)]
  transfers between devices with their start and end apart: 4 -> 5, of which waited for: 3 -> 4; matrix products, arithmetic and copies ran while one was open for 6% -> 6% of each run, Pallas kernels for 0% -> 0%
where the time goes in v1:
time: 378 us; the launch traced here: 374 us
  waiting for transfers between devices  123 us (33%)
  matrix products  110 us (29%)
  starting transfers between devices  43.2 us (11%)
  local copies, waits for them, and re-layouts  43.1 us (11%)
  other arithmetic  33.1 us (9%)
  between operations  13.7 us (4%)
  blocking collectives  8.23 us (2%)
    all_gather x2, waiting for transfers between devices, by_axis(): x = jnp.sum(lax.all_gather(x, axis), axis=0)  98.4 us
    dot_general x16, matrix products, update(): jnp.einsum('bsh,shk->bhk', factor, slot_out)  42.6 us
    dot_general x16, matrix products, update(): jnp.einsum('sht,stk->shk', exponent.astype(jnp.bfloat16), latent_block, p...  24.3 us
    dot_general x16, matrix products, update(): jnp.einsum('shk,stk->sht', pick_latent, latent_block, preferred_element_t...  22 us
    all_to_all x1, starting transfers between devices, from_everyone(): lax.all_to_all(jnp.broadcast_to(x[None], (size, *x.shape)), axis, 0, 0, t...  21.8 us
    all_to_all x1, waiting for transfers between devices, local(): lax.all_to_all(run_out, SEQ, split_axis=2, concat_axis=2, tiled=True)  18.9 us
    dynamic_slice x16, local copies, waits for them, and re-layouts, update(): lax.dynamic_slice_in_dim(rope_cache, start, 8, 0)  13.5 us
    all_to_all x1, starting transfers between devices, side_by_side(): lax.all_to_all(both, axis, split_axis=split_dim, concat_axis=concat_dim,...  13.3 us
  transfers between devices with their start and end apart: 5, of which 4 were waited for; matrix products, arithmetic and copies ran while one was open for 6% of the time, Pallas kernels for 0%

profile of v1, /device:TPU:513, one launch (start us, length us, event | category | flops | bytes accessed | tf_op | source)
XLA Modules:
  0.0 374.5 jit_solution(5219496305210417585)
XLA Ops:
  9.8 21.8 %all-to-all-start = ((bf16[64,2,2048]{2,1,0:T(2,128)(2,1)}), bf16[64,2,2048]{2,1,0:T(2,128)(2,1)}, u32[]{:S(2)}, u32[]{:S(2)}) async-start(bf16[64,2,2048]{2,1,0:T(2,128)(2,1)} %reshape.122), calls=%async_computation | async-start | bytes 1048576 | tf_op jit(solution)/shard_map/all_to_all | solution.py:21
  31.9 5.7 %fusion.41 = pred[8,128]{1,0:T(8,128)(4,1)S(1)} fusion(s32[8,2048]{1,0:T(8,128)S(1)} %get-tuple-element.279, pred[8,2048]{1,0:T(8,128)(4,1)S(1)} %iota_compare_fusion.2), kind=kLoop, calls=%fused_computation.56 | loop fusion | flops 6290432 | bytes 82944 | tf_op jit(solution)/shard_map/reduce_or | solution.py:81
  37.7 7.8 %select_reduce_fusion.2 = s32[128]{0:T(128)S(1)} fusion(s32[8,2048]{1,0:T(8,128)S(1)} %get-tuple-element.278, s32[8,2048]{1,0:T(8,128)S(1)} %get-tuple-element.279, pred[8,2048]{1,0:T(8,128)(4,1)S(1)} %iota_compare_fusion.2), kind=kLoop, calls=%fused_computation.53 | loop fusion | flops 8388480 | bytes 147968 | tf_op jit(solution)/shard_map/reduce_sum | solution.py:82
  45.5 2.3 reshape.123
  51.0 138.7 %while.18 = (s32[]{:T(128)}, f32[8,64]{0,1:T(8,128)S(1)}, f32[8,64]{0,1:T(8,128)S(1)}, f32[8,64,512]{2,0,1:T(8,128)}, bf16[8,128]{1,0:T(8,128)(2,1)S(1)}, /*inde...) while((s32[]{:T(128)}, f32[8,64]{0,1:T(8,128)S(1)}, ...), condition=%wide.region_6.7_spmd.clone, body=%wide.region_2.6_spmd.clone.sunk | while | flops 81668672 | bytes 7003699 | solution.py:135
  64.5 2.7 fusion.93
  73.3 2.7 fusion.93
  82.0 2.7 fusion.93
  90.8 2.7 fusion.93
  99.5 2.7 fusion.93
  108.2 2.7 fusion.93
  117.0 2.7 fusion.93
  125.7 2.7 fusion.93
  134.5 2.7 fusion.93
  143.2 2.7 fusion.93
  151.9 2.7 fusion.93
  160.7 2.7 fusion.93
  169.4 2.7 fusion.93
  178.2 2.7 fusion.93
  186.9 2.7 fusion.93
  190.9 13.3 %all-to-all-start.2 = ((f32[64,1,1024]{2,1,0:T(1,128)}), f32[64,1,1024]{2,1,0:T(1,128)S(1)}, u32[]{:S(2)}, u32[]{:S(2)}) async-start(f32[64,1,1024]{2,1,0:T(1,128)} %reshape.126), calls=%async_computation.2 | async-start | bytes 524288 | tf_op jit(solution)/shard_map/all_to_all | solution.py:36
  204.3 2.3 copy.70
  206.6 3.4 reshape.124
  210.0 5.1 %all-to-all-done.2 = f32[64,1,1024]{2,1,0:T(1,128)S(1)} async-done(((f32[64,1,1024]{2,1,0:T(1,128)}), f32[64,1,1024]{2,1,0:T(1,128)S(1)}, u32[]{:S(2)}, u32[]{:S(2)}) %all-to-all-start.2) | async-done | bytes 262176 | tf_op jit(solution)/shard_map/all_to_all | solution.py:36
  215.2 7.9 %all-to-all-start.1 = ((f32[64,1,4096]{2,1,0:T(1,128)}), f32[64,1,4096]{2,1,0:T(1,128)}, u32[]{:S(2)}, u32[]{:S(2)}) async-start(f32[64,1,4096]{2,1,0:T(1,128)} %reshape.124), calls=%async_computation.1 | async-start | bytes 2097152 | tf_op jit(solution)/shard_map/all_to_all | solution.py:142
  225.3 18.9 %all-to-all-done.1 = f32[64,1,4096]{2,1,0:T(1,128)} async-done(((f32[64,1,4096]{2,1,0:T(1,128)}), f32[64,1,4096]{2,1,0:T(1,128)}, u32[]{:S(2)}, u32[]{:S(2)}) %all-to-all-start.1) | async-done | bytes 1048608 | tf_op jit(solution)/shard_map/all_to_all | solution.py:142
  244.2 4.4 %reduce = f32[64,4096]{1,0:T(8,128)S(1)} reduce(f32[64,1,4096]{2,1,0:T(1,128)} %all-to-all-done.1, f32[]{:T(128)} %broadcast.134), dimensions={1}, to_apply=%all_to_all.13.reduce_sub_computation | reduce | bytes 2097156 | tf_op jit(solution)/shard_map/all_to_all | solution.py:142
  248.6 2.2 reshape.125
  250.7 2.2 fusion.42
  254.2 56.2 %all-gather.5.cloned.1.call-done = f32[64,64,128]{2,0,1:T(8,128)} async-done(((f32[8,64,128]{2,0,1:T(8,128)}), f32[64,64,128]{2,0,1:T(8,128)}) %all-gather.5.cloned.1.call-update) | async-done | bytes 2097168 | tf_op jit(solution)/shard_map/all_gather | solution.py:45
  313.1 42.2 %all-gather.7.cloned.1.call-done = f32[64,64,128]{2,1,0:T(8,128)} async-done(((f32[8,64,128]{2,1,0:T(8,128)}), f32[64,64,128]{2,1,0:T(8,128)}) %all-gather.7.cloned.1.call-update) | async-done | bytes 2097168 | tf_op jit(solution)/shard_map/all_gather | solution.py:45
  358.1 8.2 %all_to_all.20 = f32[2,1,448]{2,1,0:T(1,128)S(1)} all-to-all(f32[2,1,448]{2,1,0:T(1,128)S(1)} %reshape.128), channel_id=1, replica_groups=mesh['groups'=2,'seq_0'=8,'seq_1'=8,'mp'=2] {'mp'}, dimensions={0} | all-to-all | bytes 7168 | tf_op jit(solution)/shard_map/all_to_all | solution.py:57
  (393 shorter events, 114.7 us)
Async XLA Ops:
  6.5 350.5 %copy-start = (bf16[8192,112]{0,1:T(8,128)(2,1)S(1)}, bf16[8192,112]{0,1:T(8,128)(2,1)}, u32[]{:S(2)}) copy-start(bf16[8192,112]{0,1:T(8,128)(2,1)} %param.17) | copy-start | bytes 5505028
  6.6 25.2 %copy-start.5 = (s32[8]{0:T(128)S(1)}, s32[8]{0:T(128)}, u32[]{:S(2)}) copy-start(s32[8]{0:T(128)} %param.19) | copy-start | bytes 100
  6.6 25.2 %copy-start.4 = (s32[8,2048]{1,0:T(8,128)S(1)}, s32[8,2048]{1,0:T(8,128)}, u32[]{:S(2)}) copy-start(s32[8,2048]{1,0:T(8,128)} %param.18) | copy-start | bytes 196612
  7.9 29.8 %copy-start.2 = (bf16[8,64,64]{2,1,0:T(8,128)(2,1)S(1)}, bf16[8,64,64]{2,1,0:T(8,128)(2,1)}, u32[]{:S(2)}) copy-start(bf16[8,64,64]{2,1,0:T(8,128)(2,1)} %param.14) | copy-start | bytes 196612
  9.8 35.7 %all-to-all-start = ((bf16[64,2,2048]{2,1,0:T(2,128)(2,1)}), bf16[64,2,2048]{2,1,0:T(2,128)(2,1)}, u32[]{:S(2)}, u32[]{:S(2)}) async-start(bf16[64,2,2048]{2,1,0:T(2,128)(2,1)} %reshape.122), calls=%async_computation | async-start | bytes 1048576 | tf_op jit(solution)/shard_map/all_to_all | solution.py:21
  189.6 14.6 %copy-start.1 = (f32[8,64,512]{2,0,1:T(8,128)S(1)}, f32[8,64,512]{2,0,1:T(8,128)}, u32[]{:S(2)}) copy-start(f32[8,64,512]{2,0,1:T(8,128)} %get-tuple-element.176) | copy-start | bytes 3145732
  190.9 24.2 %all-to-all-start.2 = ((f32[64,1,1024]{2,1,0:T(1,128)}), f32[64,1,1024]{2,1,0:T(1,128)S(1)}, u32[]{:S(2)}, u32[]{:S(2)}) async-start(f32[64,1,1024]{2,1,0:T(1,128)} %reshape.126), calls=%async_computation.2 | async-start | bytes 524288 | tf_op jit(solution)/shard_map/all_to_all | solution.py:36
  215.2 29.0 %all-to-all-start.1 = ((f32[64,1,4096]{2,1,0:T(1,128)}), f32[64,1,4096]{2,1,0:T(1,128)}, u32[]{:S(2)}, u32[]{:S(2)}) async-start(f32[64,1,4096]{2,1,0:T(1,128)} %reshape.124), calls=%async_computation.1 | async-start | bytes 2097152 | tf_op jit(solution)/shard_map/all_to_all | solution.py:142
  223.1 87.3 %all-gather.5.cloned.1.call-start = ((), (), s32[]{:S(2)}) async-start(), calls=%async_computation.4 | async-start | bytes 2359296 | tf_op jit(solution)/shard_map/all_gather | solution.py:45
  248.5 4.5 %copy-start.3 = (bf16[64,8,128]{2,1,0:T(8,128)(2,1)S(1)}, bf16[64,8,128]{2,1,0:T(8,128)(2,1)}, u32[]{:S(2)}) copy-start(bf16[64,8,128]{2,1,0:T(8,128)(2,1)} %param.16) | copy-start | bytes 393220
  254.1 101.1 %all-gather.7.cloned.1.call-start = ((), (), s32[]{:S(2)}) async-start(), calls=%async_computation.5 | async-start | bytes 2359296 | tf_op jit(solution)/shard_map/all_gather | solution.py:45
Sparse Core Ops, SparseCore 0:
  254.2 56.1 all-gather.4
  313.2 41.9 all-gather.6
